TPU v7x, 128 devices: a whole 4x4x4 slice. The times are simulated.
128 devices in a mesh: sim: 32 (over z, y, x_hi), learn: 4 (over x_lo, core).
Axes of the slice: x: 4 (x_hi: 2, x_lo: 2; x = x_hi * 2 + x_lo), y: 4, z: 4, core: 2. Of those that a mesh axis runs over, the one named last changes fastest.
Arguments:
- state_field: float32 [128, 512, 2048], P(None, 'sim', 'learn'), may hold values from -6 to 6
- diffusion: float32 [128], replicated, may hold values from 0.03 to 0.24
- weight_in: float32 [128, 1024], replicated, may hold values from -0.5 to 0.5
- weight_mid: float32 [1024, 1024], replicated, may hold values from -0.1875 to 0.1875
- weight_out: float32 [1024, 128], replicated, may hold values from -0.1875 to 0.1875
- block_tile: int32 [1536, 1], P('learn'), may hold values from 0 to 31; in each aligned block of 12 rows (0 to 11, 12 to 23, ...) no two rows name the same one
- block_pos: int32 [1536], P('learn'), may hold values from 0 to 63
Outputs:
- new_state: float32 [128, 512, 2048], P(None, 'sim', 'learn')
- new_in: float32 [128, 1024], replicated
- new_mid: float32 [1024, 1024], replicated
- new_out: float32 [1024, 128], replicated
Inputs may be any that keep to these rules, and one draw needn't show every extreme that they name: `block_tile`: in each aligned block of 12 rows no tile index appears twice.
All inputs are finite; a program needn't handle non-finite values.
Results may differ from a plain program's by a relative error of at most 0.0003.
The roundings to bfloat16 on the way count: a program that leaves them out, or rounds other values in their place, can miss the bound.
Values may be sent and summed in bfloat16 or wider, within the bound.
No kernel may reach another device: no remote copies, remote signals or barrier semaphores. Data moves between devices by JAX's collectives and lax.ppermute only.
A program may use at most 128 MiB of HBM per device.

v0:
```python
import jax
import jax.numpy as jnp
from jax import lax
from jax.sharding import PartitionSpec as P

BW = 128
RATE = 0.5
TARGET_GAIN = 4.0


def with_halo(x, sides, width):
    for axis, dim in sides:
        size, length = (lax.axis_size(axis), x.shape[dim])
        up = [(i, (i + 1) % size) for i in range(size)]
        down = [(j, i) for i, j in up]
        last = lax.slice_in_dim(x, length - width, length, axis=dim)
        first = lax.slice_in_dim(x, 0, width, axis=dim)
        before = lax.ppermute(last, axis, up)
        after = lax.ppermute(first, axis, down)
        x = jnp.concatenate([before, x, after], axis=dim)
    return x


def interior_step(padded, diffusion):
    center = padded[:, 1:-1, 1:-1]
    beside_all = padded[:, :-2, 1:-1] + padded[:, 2:, 1:-1]
    beside_all = beside_all + padded[:, 1:-1, :-2] + padded[:, 1:-1, 2:]
    return center + diffusion[:, None, None] * (beside_all - 4.0 * center)


def silu_slope(value):
    sigma = jax.nn.sigmoid(value)
    return sigma * (1.0 + value * (1.0 - sigma))


def gradients(inputs, targets, weight_in, weight_mid, weight_out, count):
    first = weight_in.astype(jnp.bfloat16)
    second = weight_mid.astype(jnp.bfloat16)
    third = weight_out.astype(jnp.bfloat16)
    pre_one = jnp.dot(inputs, first, preferred_element_type=jnp.float32)
    act_one = jax.nn.silu(pre_one).astype(jnp.bfloat16)
    pre_two = jnp.dot(act_one, second, preferred_element_type=jnp.float32)
    act_two = jax.nn.silu(pre_two).astype(jnp.bfloat16)
    output = jnp.dot(act_two, third, preferred_element_type=jnp.float32)
    error = ((output - targets.astype(jnp.float32)) / count).astype(jnp.bfloat16)
    grad_out = jnp.dot(act_two.T, error, preferred_element_type=jnp.float32)
    back_two = jnp.dot(error, third.T, preferred_element_type=jnp.float32)
    delta_two = (back_two * silu_slope(pre_two)).astype(jnp.bfloat16)
    grad_mid = jnp.dot(act_one.T, delta_two, preferred_element_type=jnp.float32)
    back_one = jnp.dot(delta_two, second.T, preferred_element_type=jnp.float32)
    delta_one = (back_one * silu_slope(pre_one)).astype(jnp.bfloat16)
    grad_in = jnp.dot(inputs.T, delta_one, preferred_element_type=jnp.float32)
    return (grad_in, grad_mid, grad_out)


def on_device(state_field, diffusion, weight_in, weight_mid, weight_out, block_tile, block_pos):
    levels, tile_rows, tile_cols = state_field.shape
    padded = with_halo(state_field, (("sim", 1), ("learn", 2)), 2)
    after = interior_step(interior_step(padded, diffusion), diffusion)
    increment = after - state_field
    senders = lax.axis_size("sim")
    own_index = lax.axis_index("sim")
    samples = block_tile.shape[0] // senders
    per_row = tile_cols // BW
    tiles = block_tile[:, 0].reshape(senders, samples)
    places = block_pos.reshape(senders, samples)
    matched = tiles == own_index
    place = jnp.sum(jnp.where(matched, places, 0), axis=1)
    present = jnp.any(matched, axis=1)

    def cut(spot):
        row = spot // per_row
        start = spot % per_row * BW
        zero = jnp.zeros((), jnp.int32)
        piece_in = lax.dynamic_slice(state_field, (zero, row, start), (levels, 1, BW))[:, 0, :]
        piece_target = lax.dynamic_slice(increment, (zero, row, start), (levels, 1, BW))[:, 0, :]
        return (piece_in, piece_target)

    cols_in, cols_target = jax.vmap(cut)(place)
    keep = present[:, None, None]
    send_in = jnp.where(keep, jnp.swapaxes(cols_in, 1, 2), 0.0).astype(jnp.bfloat16)
    send_target = jnp.where(keep, TARGET_GAIN * jnp.swapaxes(cols_target, 1, 2), 0.0).astype(
        jnp.bfloat16
    )
    got_in, got_target = (
        lax.all_to_all(send_in, "sim", split_axis=0, concat_axis=0, tiled=True),
        lax.all_to_all(send_target, "sim", split_axis=0, concat_axis=0, tiled=True),
    )
    wanted = lax.dynamic_slice_in_dim(tiles, own_index, 1, 0)[0]
    inputs = jnp.take(got_in, wanted, axis=0).reshape(-1, levels)
    targets = jnp.take(got_target, wanted, axis=0).reshape(-1, levels)
    count = float(senders * lax.axis_size("learn") * samples * BW)
    grad_in, grad_mid, grad_out = gradients(
        inputs, targets, weight_in, weight_mid, weight_out, count
    )
    total_in, total_mid, total_out = lax.psum((grad_in, grad_mid, grad_out), ("sim", "learn"))
    new_in = weight_in - RATE * total_in
    new_mid = weight_mid - RATE * total_mid
    new_out = weight_out - RATE * total_out
    return (after, new_in, new_mid, new_out)


def solution(mesh):
    placed = (P(None, "sim", "learn"), P(), P(), P(), P(), P("learn", None), P("learn"))
    return jax.shard_map(
        on_device,
        mesh=mesh,
        in_specs=placed,
        out_specs=(P(None, "sim", "learn"), P(), P(), P()),
        check_vma=False,
    )
```

profile of v0, /device:TPU:1, one launch (start us, length us, event | category | flops | bytes accessed | tf_op | source)
XLA Modules:
  0.0 309.1 jit_solution(2728969360066584125)
XLA Ops:
  7.2 0.0 copy-start.9
  7.2 0.0 copy-start.7
  7.2 5.8 %copy.26 = f32[128,16,512]{0,1,2:T(8,128)} copy(f32[128,16,512]{2,1,0:T(8,128)} %param.9) | data formatting | bytes 8388608 | tf_op args[0]
  13.0 2.6 fusion.34
  15.6 3.6 %collective-permute-start = (f32[128,2,512]{0,1,2:T(2,128)S(1)}, f32[128,2,512]{0,1,2:T(2,128)S(1)}, u32[]{:S(2)}, u32[]{:S(2)}) collective-permute-start(f32[128,2,512]{0,1,2:T(2,128)S(1)} %get-tuple-element.28), channel_id=1, source_target_pairs={{0,4},{4,8},{8,12},{12,16},{16,20},{20,24},{24,28},{28,32},{32,36}... | collective-permute-start | bytes 1572872 | tf_op jit(solution)/shard_map/ppermute | solution.py:18
  19.2 6.0 %collective-permute-start.1 = (f32[128,2,512]{0,1,2:T(2,128)S(1)}, f32[128,2,512]{0,1,2:T(2,128)S(1)}, u32[]{:S(2)}, u32[]{:S(2)}) collective-permute-start(f32[128,2,512]{0,1,2:T(2,128)S(1)} %get-tuple-element.29), channel_id=1, source_target_pairs={{4,0},{8,4},{12,8},{16,12},{20,16},{24,20},{28,24},{32,28},{36,32}... | collective-permute-start | bytes 1572872 | tf_op jit(solution)/shard_map/ppermute | solution.py:19
  25.2 0.0 copy-done.9
  25.2 0.1 reshape_squeeze.3
  25.3 0.0 copy-done.7
  25.4 0.1 reshape.119
  25.5 0.1 fusion.33
  25.6 0.1 select_reduce_fusion
  25.7 6.1 %gather_fusion = bf16[32,128,128]{1,0,2:T(8,128)(2,1)S(1)} fusion(f32[128,16,512]{0,1,2:T(8,128)} %copy.26, s32[32]{0:T(128)S(1)} %fusion.28), kind=kCustom, calls=%fused_computation.2 | custom fusion | bytes 2097536 | tf_op jit(solution)/shard_map/vmap()/gather | solution.py:75
  31.8 4.9 %collective-permute-done = f32[128,2,512]{0,1,2:T(2,128)S(1)} collective-permute-done((f32[128,2,512]{0,1,2:T(2,128)S(1)}, f32[128,2,512]{0,1,2:T(2,128)S(1)}, u32[]{:S(2)}, u32[]{:S(2)}) %collective-permute-start) | collective-permute-done | bytes 524320 | tf_op jit(solution)/shard_map/ppermute | solution.py:18
  36.8 6.3 %collective-permute-done.1 = f32[128,2,512]{0,1,2:T(2,128)S(1)} collective-permute-done((f32[128,2,512]{0,1,2:T(2,128)S(1)}, f32[128,2,512]{0,1,2:T(2,128)S(1)}, u32[]{:S(2)}, u32[]{:S(2)}) %collective-permute-start.1) | collective-permute-done | bytes 524320 | tf_op jit(solution)/shard_map/ppermute | solution.py:19
  43.0 0.7 pad_maximum_fusion.9
  43.8 2.7 collective-permute-start.2
  46.5 0.0 collective-permute-start.3
  46.5 0.3 fusion.12
  46.8 1.4 copy.30
  48.1 10.2 %all-to-all-start = ((bf16[32,128,128]{2,1,0:T(8,128)(2,1)}), bf16[32,128,128]{2,1,0:T(8,128)(2,1)}, u32[]{:S(2)}, u32[]{:S(2)}) async-start(bf16[32,128,128]{2,1,0:T(8,128)(2,1)} %copy.30), calls=%async_computation | async-start | bytes 2097152 | tf_op jit(solution)/shard_map/all_to_all | solution.py:86
  58.4 0.0 copy-start
  58.4 0.0 copy-start.8
  58.4 0.0 collective-permute-done.2
  58.4 0.0 collective-permute-done.3
  58.4 4.3 %pad_maximum_fusion = f32[128,20,516]{0,1,2:T(8,128)S(1)} fusion(f32[128,20,2]{0,1,2:T(8,128)S(1)} %collective-permute-done.3, f32[128,2,512]{0,1,2:T(2,128)S(1)} %collective-permute-done.1, f32[128,16,512]{0,1,2:T(8,128)} %copy.26, f32[128,2,512]{0,1,2:T(2,128)S(1)} %collective-permute-done, f32[128,20,2]{0,1,2:T(8,128)S(1)} %collective-permute-done.2), kind=kLoop, calls=%fused_computation.4 | loop fusion | flops 5283840 | bytes 10567680 | tf_op jit(solution)/shard_map/concatenate | solution.py:20
  62.7 0.0 copy-done
  62.7 0.0 copy-done.8
  62.7 7.1 %fusion.3 = f32[128,18,514]{0,1,2:T(8,128)S(1)} fusion(f32[128,20,2]{0,1,2:T(8,128)S(1)} %collective-permute-done.3, f32[128,2,512]{0,1,2:T(2,128)S(1)} %collective-permute-done.1, f32[128,16,512]{0,1,2:T(8,128)S(1)} %copy-done, f32[128,2,512]{0,1,2:T(2,128)S(1)} %collective-permute-done, f32[128,20,2]{0,1,2:T(8,128)S(1)} %collective-permute-done.2, ...), kind=kLoop, calls=%fused_computation.9 | loop fusion | flops 15395328 | bytes 24232448 | tf_op jit(solution)/shard_map/add | solution.py:28
  69.8 4.7 %fusion.31 = (f32[128,16,512]{0,1,2:T(8,128)}, f32[128,16,512]{0,1,2:T(8,128)}) fusion(f32[128,16,512]{0,1,2:T(8,128)S(1)} %copy-done, f32[128,18,514]{0,1,2:T(8,128)S(1)} %fusion.3, f32[128]{0:T(128)S(1)} %copy-done.8), kind=kLoop, calls=%fused_computation.75 | loop fusion | flops 8388608 | bytes 33554944 | tf_op jit(solution)/shard_map/sub | solution.py:60
  74.5 6.1 %gather_fusion.1 = f32[32,128,128]{1,0,2:T(8,128)S(1)} fusion(f32[128,16,512]{0,1,2:T(8,128)} %get-tuple-element.20, s32[32]{0:T(128)S(1)} %fusion.28), kind=kCustom, calls=%fused_computation.3 | custom fusion | bytes 4194688 | tf_op jit(solution)/shard_map/vmap()/gather | solution.py:76
  80.6 0.0 copy-start.4
  80.6 0.4 fusion.13
  81.0 1.4 copy.32
  82.3 0.0 all-to-all-done
  82.3 9.1 %all-to-all-start.1 = ((bf16[32,128,128]{2,1,0:T(8,128)(2,1)}), bf16[32,128,128]{2,1,0:T(8,128)(2,1)S(1)}, u32[]{:S(2)}, u32[]{:S(2)}) async-start(bf16[32,128,128]{2,1,0:T(8,128)(2,1)} %copy.32), calls=%async_computation.1 | async-start | bytes 2097152 | tf_op jit(solution)/shard_map/all_to_all | solution.py:87
  91.4 0.3 all-reduce.3.cloned.1.call-start
  91.7 1.8 gather_fusion.2
  93.6 14.9 %all-to-all-done.1 = bf16[32,128,128]{2,1,0:T(8,128)(2,1)S(1)} async-done(((bf16[32,128,128]{2,1,0:T(8,128)(2,1)}), bf16[32,128,128]{2,1,0:T(8,128)(2,1)S(1)}, u32[]{:S(2)}, u32[]{:S(2)}) %all-to-all-start.1) | async-done | bytes 1048608 | tf_op jit(solution)/shard_map/all_to_all | solution.py:87
  108.5 0.6 gather_fusion.3
  109.1 0.0 copy-start.2
  109.1 0.1 broadcast_select_fusion
  109.3 0.0 copy-done.4
  109.3 1.0 fusion.18
  110.3 1.1 copy-done.2
  111.3 0.0 copy-start.1
  111.3 4.5 %multiply_convert_fusion.2 = (bf16[1536,1024]{1,0:T(8,128)(2,1)S(1)}, f32[1536,1024]{1,0:T(8,128)S(1)}) fusion(f32[1024,1024]{1,0:T(8,128)S(1)} %copy-done.2, f32[1536,1024]{1,0:T(8,128)S(1)} %fusion.18), kind=kOutput, calls=%fused_computation.19 | convolution fusion | flops 3238002688 | bytes 19922944 | tf_op jit(solution)/shard_map/dot_general | solution.py:42
  115.9 0.0 copy-done.3
  115.9 1.0 fusion.9
  116.9 1.8 fusion.35
  118.7 2.7 multiply_convert_fusion.1
  121.4 0.0 copy-done.1
  121.4 0.0 copy-start.10
  121.4 1.7 copy-done.10
  123.1 5.1 %fusion.30 = f32[1024,1024]{1,0:T(8,128)} fusion(bf16[1536,1024]{1,0:T(8,128)(2,1)S(1)} %multiply_convert_fusion.1, f32[1536,1024]{1,0:T(8,128)S(1)} %fusion.18), kind=kOutput, calls=%fused_computation.74 | convolution fusion | flops 3229089792 | bytes 13631488 | tf_op jit(solution)/shard_map/dot_general | solution.py:49
  128.2 10.6 %fusion.11 = f32[128,1024]{1,0:T(8,128)} fusion(bf16[1536,128]{1,0:T(8,128)(2,1)S(1)} %bitcast.36, f32[1536,1024]{1,0:T(8,128)} %copy-done.1, bf16[1536,1024]{1,0:T(8,128)(2,1)} %copy-done.10, f32[1024,1024]{1,0:T(8,128)} %param.12), kind=kOutput, calls=%fused_computation.36 | convolution fusion | flops 3639083008 | bytes 14548992 | tf_op jit(solution)/shard_map/dot_general | solution.py:52
  138.8 0.0 all-reduce.3.cloned.1.call-update
  138.8 5.6 %copy.33 = f32[128,16,512]{2,1,0:T(8,128)} copy(f32[128,16,512]{0,1,2:T(8,128)} %get-tuple-element.21) | data formatting | bytes 8388608
  144.3 149.3 %all-reduce.3.cloned.1.call-done = (f32[128,1024]{1,0:T(8,128)}, f32[1024,1024]{1,0:T(8,128)}, f32[1024,128]{1,0:T(8,128)}) async-done(((f32[128,1024]{1,0:T(8,128)}, f32[1024,1024]{1,0:T(8,128)}, f32[1024,128]{1,0:T(8,128)}), (f32[128,1024]{1,0:T(8,128)}, f32[1024,1024]{1,0:T(8,128)}, f32[1024,128]{1,0:T(8,128)})) %all-reduce.3.cloned.1.call-update) | async-done | bytes 5242896 | tf_op jit(solution)/shard_map/psum | solution.py:96
  293.6 7.0 %multiply_subtract_fusion = f32[1024,1024]{1,0:T(8,128)} fusion(f32[1024,1024]{1,0:T(8,128)} %param.12, f32[1024,1024]{1,0:T(8,128)} %get-tuple-element.18), kind=kLoop, calls=%fused_computation.29 | loop fusion | flops 2097152 | bytes 12582912 | tf_op jit(solution)/shard_map/sub | solution.py:98
  300.6 0.0 copy-done.6
  300.6 0.8 multiply_subtract_fusion.1
  301.4 0.0 copy-done.5
  301.4 0.9 multiply_subtract_fusion.2
  (7 shorter events, 0.1 us)
Async XLA Ops:
  7.2 18.1 %copy-start.9 = (s32[384,1]{0,1:T(1,128)S(1)}, s32[384,1]{0,1:T(1,128)}, u32[]{:S(2)}) copy-start(s32[384,1]{0,1:T(1,128)} %param.14) | copy-start | bytes 4612
  7.2 18.2 %copy-start.7 = (s32[384]{0:T(512)S(1)}, s32[384]{0:T(512)}, u32[]{:S(2)}) copy-start(s32[384]{0:T(512)} %param.15) | copy-start | bytes 4612
  15.6 21.2 %collective-permute-start = (f32[128,2,512]{0,1,2:T(2,128)S(1)}, f32[128,2,512]{0,1,2:T(2,128)S(1)}, u32[]{:S(2)}, u32[]{:S(2)}) collective-permute-start(f32[128,2,512]{0,1,2:T(2,128)S(1)} %get-tuple-element.28), channel_id=1, source_target_pairs={{0,4},{4,8},{8,12},{12,16},{16,20},{20,24},{24,28},{28,32},{32,36}... | collective-permute-start | bytes 1572872 | tf_op jit(solution)/shard_map/ppermute | solution.py:18
  19.2 23.8 %collective-permute-start.1 = (f32[128,2,512]{0,1,2:T(2,128)S(1)}, f32[128,2,512]{0,1,2:T(2,128)S(1)}, u32[]{:S(2)}, u32[]{:S(2)}) collective-permute-start(f32[128,2,512]{0,1,2:T(2,128)S(1)} %get-tuple-element.29), channel_id=1, source_target_pairs={{4,0},{8,4},{12,8},{16,12},{20,16},{24,20},{28,24},{32,28},{36,32}... | collective-permute-start | bytes 1572872 | tf_op jit(solution)/shard_map/ppermute | solution.py:19
  43.8 14.6 %collective-permute-start.2 = (f32[128,20,2]{0,1,2:T(8,128)S(1)}, f32[128,20,2]{0,1,2:T(8,128)S(1)}, u32[]{:S(2)}, u32[]{:S(2)}) collective-permute-start(f32[128,20,2]{0,1,2:T(8,128)S(1)} %get-tuple-element.26), channel_id=1, source_target_pairs={{0,1},{1,2},{2,3},{3,0},{4,5},{5,6},{6,7},{7,4},{8,9},{9,10},{10,1... | collective-permute-start | bytes 61448 | tf_op jit(solution)/shard_map/ppermute | solution.py:18
  46.5 11.9 %collective-permute-start.3 = (f32[128,20,2]{0,1,2:T(8,128)S(1)}, f32[128,20,2]{0,1,2:T(8,128)S(1)}, u32[]{:S(2)}, u32[]{:S(2)}) collective-permute-start(f32[128,20,2]{0,1,2:T(8,128)S(1)} %get-tuple-element.27), channel_id=1, source_target_pairs={{1,0},{2,1},{3,2},{0,3},{5,4},{6,5},{7,6},{4,7},{9,8},{10,9},{11,1... | collective-permute-start | bytes 61448 | tf_op jit(solution)/shard_map/ppermute | solution.py:19
  48.1 34.2 %all-to-all-start = ((bf16[32,128,128]{2,1,0:T(8,128)(2,1)}), bf16[32,128,128]{2,1,0:T(8,128)(2,1)}, u32[]{:S(2)}, u32[]{:S(2)}) async-start(bf16[32,128,128]{2,1,0:T(8,128)(2,1)} %copy.30), calls=%async_computation | async-start | bytes 2097152 | tf_op jit(solution)/shard_map/all_to_all | solution.py:86
  58.4 4.3 %copy-start = (f32[128,16,512]{0,1,2:T(8,128)S(1)}, f32[128,16,512]{0,1,2:T(8,128)}, u32[]{:S(2)}) copy-start(f32[128,16,512]{0,1,2:T(8,128)} %copy.26) | copy-start | bytes 12582916
  58.4 4.3 %copy-start.8 = (f32[128]{0:T(128)S(1)}, f32[128]{0:T(128)}, u32[]{:S(2)}) copy-start(f32[128]{0:T(128)} %param.10) | copy-start | bytes 1540
  80.6 28.7 %copy-start.4 = (f32[128,1024]{1,0:T(8,128)S(1)}, f32[128,1024]{1,0:T(8,128)}, u32[]{:S(2)}) copy-start(f32[128,1024]{1,0:T(8,128)} %param.11) | copy-start | bytes 1572868
  82.3 26.2 %all-to-all-start.1 = ((bf16[32,128,128]{2,1,0:T(8,128)(2,1)}), bf16[32,128,128]{2,1,0:T(8,128)(2,1)S(1)}, u32[]{:S(2)}, u32[]{:S(2)}) async-start(bf16[32,128,128]{2,1,0:T(8,128)(2,1)} %copy.32), calls=%async_computation.1 | async-start | bytes 2097152 | tf_op jit(solution)/shard_map/all_to_all | solution.py:87
  91.4 202.2 %all-reduce.3.cloned.1.call-start = ((), (), s32[]{:S(2)}) async-start(), calls=%async_computation.2 | async-start | bytes 10485760 | tf_op jit(solution)/shard_map/psum | solution.py:96
  109.1 2.2 copy-start.2
  111.3 10.1 %copy-start.1 = (f32[1536,1024]{1,0:T(8,128)}, f32[1536,1024]{1,0:T(8,128)S(1)}, u32[]{:S(2)}) copy-start(f32[1536,1024]{1,0:T(8,128)S(1)} %fusion.18) | copy-start | bytes 18874372
  111.3 4.6 %copy-start.3 = (f32[1024,128]{1,0:T(8,128)S(1)}, f32[1024,128]{1,0:T(8,128)}, u32[]{:S(2)}) copy-start(f32[1024,128]{1,0:T(8,128)} %param.13) | copy-start | bytes 1572868
  121.4 1.7 copy-start.10
  293.6 7.0 %copy-start.6 = (f32[1024,128]{1,0:T(8,128)S(1)}, f32[1024,128]{1,0:T(8,128)}, u32[]{:S(2)}) copy-start(f32[1024,128]{1,0:T(8,128)} %get-tuple-element.19) | copy-start | bytes 1572868
  293.6 7.8 %copy-start.5 = (f32[128,1024]{1,0:T(8,128)S(1)}, f32[128,1024]{1,0:T(8,128)}, u32[]{:S(2)}) copy-start(f32[128,1024]{1,0:T(8,128)} %get-tuple-element.17) | copy-start | bytes 1572868
Sparse Core Ops, SparseCore 0:
  138.9 154.6 all-reduce.2
where the time goes:
time: 310 us; the launch traced here: 309 us
  waiting for transfers between devices  175 us (56%)
  local copies, waits for them, and re-layouts  34.3 us (11%)
  starting transfers between devices  31.9 us (10%)
  matrix products  26.7 us (9%)
  other arithmetic  26.5 us (9%)
  between operations  14.3 us (5%)
    psum x1, waiting for transfers between devices, on_device(): lax.psum((grad_in, grad_mid, grad_out), ('sim', 'learn'))  149 us
    all_to_all x1, waiting for transfers between devices, on_device(): lax.all_to_all(send_target, 'sim', split_axis=0, concat_axis=0, tiled=True)  14.9 us
    unnamed x24, local copies, waits for them, and re-layouts  14.1 us
    dot_general x1, matrix products, gradients(): grad_in = jnp.dot(inputs.T, delta_one, preferred_element_type=jnp.float32)  10.6 us
    all_to_all x1, starting transfers between devices, on_device(): lax.all_to_all(send_in, 'sim', split_axis=0, concat_axis=0, tiled=True)  10.2 us
    all_to_all x1, starting transfers between devices, on_device(): lax.all_to_all(send_target, 'sim', split_axis=0, concat_axis=0, tiled=True)  9.08 us
    add x1, other arithmetic, interior_step(): return center + diffusion[:, None, None] * (beside_all - 4.0 * center)  7.08 us
    sub x1, other arithmetic, on_device(): new_mid = weight_mid - RATE * total_mid  6.98 us
  transfers between devices with their start and end apart: 7, of which 4 were waited for; matrix products, arithmetic and copies ran while one was open for 13% of the time, Pallas kernels for 0%

commit v1 on v0

--- a/solution.py
+++ b/solution.py
@@ -93,7 +93,9 @@
     grad_in, grad_mid, grad_out = gradients(
         inputs, targets, weight_in, weight_mid, weight_out, count
     )
-    total_in, total_mid, total_out = lax.psum((grad_in, grad_mid, grad_out), ("sim", "learn"))
+    total_in, total_mid, total_out = lax.psum(
+        lax.psum((grad_in, grad_mid, grad_out), "learn"), "sim"
+    )
     new_in = weight_in - RATE * total_in
     new_mid = weight_mid - RATE * total_mid
     new_out = weight_out - RATE * total_out

time: 310 us -> 650 us (2.10)
  the two profiles are of different devices: /device:TPU:1 before, /device:TPU:0 now
where the time goes in v1:
time: 650 us; the launch traced here: 649 us
  waiting for transfers between devices  515 us (79%)
  local copies, waits for them, and re-layouts  34.9 us (5%)
  starting transfers between devices  32 us (5%)
  matrix products  26.7 us (4%)
  other arithmetic  26.5 us (4%)
  between operations  14.3 us (2%)
    psum x1, waiting for transfers between devices, on_device(): lax.psum(lax.psum((grad_in, grad_mid, grad_out), 'learn'), 'sim')  384 us
    psum x1, waiting for transfers between devices, on_device(): lax.psum((grad_in, grad_mid, grad_out), 'learn')  104 us
    all_to_all x1, waiting for transfers between devices, on_device(): lax.all_to_all(send_target, 'sim', split_axis=0, concat_axis=0, tiled=True)  15.9 us
    unnamed x24, local copies, waits for them, and re-layouts  14.1 us
  transfers between devices with their start and end apart: 8, of which 5 were waited for; matrix products, arithmetic and copies ran while one was open for 6% of the time, Pallas kernels for 0%

profile of v1, /device:TPU:0, one launch (start us, length us, event | category | flops | bytes accessed | tf_op | source)
XLA Modules:
  0.0 649.2 jit_solution(3756447412800132102)
XLA Ops:
  7.2 0.0 copy-start.9
  7.2 0.0 copy-start.7
  7.2 5.8 copy.26
  13.0 2.6 fusion.34
  15.6 3.2 collective-permute-start
  18.8 6.0 collective-permute-start.1
  24.8 0.0 copy-done.9
  24.8 0.1 reshape_squeeze.3
  24.9 0.0 copy-done.7
  24.9 0.1 reshape.119
  25.0 0.1 fusion.33
  25.2 0.1 select_reduce_fusion
  25.3 6.4 gather_fusion
  31.7 5.8 collective-permute-done
  37.5 5.7 collective-permute-done.1
  43.2 0.7 pad_maximum_fusion.9
  43.9 0.1 collective-permute-start.2
  44.0 1.7 collective-permute-start.3
  45.7 0.3 fusion.12
  46.0 1.4 copy.30
  47.4 10.8 %all-to-all-start = ((bf16[32,128,128]{2,1,0:T(8,128)(2,1)}), bf16[32,128,128]{2,1,0:T(8,128)(2,1)}, u32[]{:S(2)}, u32[]{:S(2)}) async-start(bf16[32,128,128]{2,1,0:T(8,128)(2,1)} %copy.30), calls=%async_computation | async-start | bytes 2097152 | tf_op jit(solution)/shard_map/all_to_all | solution.py:86
  58.2 0.0 copy-start
  58.2 0.0 copy-start.8
  58.2 0.0 collective-permute-done.2
  58.3 0.0 collective-permute-done.3
  58.3 4.3 pad_maximum_fusion
  62.5 0.0 copy-done
  62.5 0.0 copy-done.8
  62.5 7.1 %fusion.3 = f32[128,18,514]{0,1,2:T(8,128)S(1)} fusion(f32[128,20,2]{0,1,2:T(8,128)S(1)} %collective-permute-done.3, f32[128,2,512]{0,1,2:T(2,128)S(1)} %collective-permute-done.1, f32[128,16,512]{0,1,2:T(8,128)S(1)} %copy-done, f32[128,2,512]{0,1,2:T(2,128)S(1)} %collective-permute-done, f32[128,20,2]{0,1,2:T(8,128)S(1)} %collective-permute-done.2, ...), kind=kLoop, calls=%fused_computation.9 | loop fusion | flops 15395328 | bytes 24232448 | tf_op jit(solution)/shard_map/add | solution.py:28
  69.6 4.7 fusion.31
  74.3 6.4 gather_fusion.1
  80.7 0.0 copy-start.4
  80.7 0.4 fusion.13
  81.1 1.4 copy.32
  82.5 0.0 all-to-all-done
  82.5 9.8 %all-to-all-start.1 = ((bf16[32,128,128]{2,1,0:T(8,128)(2,1)}), bf16[32,128,128]{2,1,0:T(8,128)(2,1)S(1)}, u32[]{:S(2)}, u32[]{:S(2)}) async-start(bf16[32,128,128]{2,1,0:T(8,128)(2,1)} %copy.32), calls=%async_computation.1 | async-start | bytes 2097152 | tf_op jit(solution)/shard_map/all_to_all | solution.py:87
  92.3 0.3 all-reduce.7.cloned.1.call-start
  92.6 1.8 gather_fusion.2
  94.5 15.9 %all-to-all-done.1 = bf16[32,128,128]{2,1,0:T(8,128)(2,1)S(1)} async-done(((bf16[32,128,128]{2,1,0:T(8,128)(2,1)}), bf16[32,128,128]{2,1,0:T(8,128)(2,1)S(1)}, u32[]{:S(2)}, u32[]{:S(2)}) %all-to-all-start.1) | async-done | bytes 1048608 | tf_op jit(solution)/shard_map/all_to_all | solution.py:87
  110.4 0.6 gather_fusion.3
  111.0 0.0 copy-start.2
  111.1 0.1 broadcast_select_fusion
  111.2 0.0 copy-done.4
  111.2 1.0 fusion.18
  112.2 1.1 copy-done.2
  113.2 4.5 multiply_convert_fusion.2
  117.8 0.0 copy-done.3
  117.8 1.0 fusion.9
  118.8 1.8 fusion.35
  120.6 2.7 multiply_convert_fusion.1
  123.3 0.0 copy-done.1
  123.3 0.0 copy-start.10
  123.3 1.7 copy-done.10
  125.0 5.1 fusion.30
  130.1 10.6 %fusion.11 = f32[128,1024]{1,0:T(8,128)} fusion(bf16[1536,128]{1,0:T(8,128)(2,1)S(1)} %bitcast.36, f32[1536,1024]{1,0:T(8,128)} %copy-done.1, bf16[1536,1024]{1,0:T(8,128)(2,1)} %copy-done.10, f32[1024,1024]{1,0:T(8,128)} %param.12), kind=kOutput, calls=%fused_computation.36 | convolution fusion | flops 3639083008 | bytes 14548992 | tf_op jit(solution)/shard_map/dot_general | solution.py:52
  140.7 0.0 all-reduce.7.cloned.1.call-update
  140.7 0.0 all-reduce.5.cloned.1.call-start
  140.7 103.5 %all-reduce.7.cloned.1.call-done = (f32[128,1024]{1,0:T(8,128)}, f32[1024,1024]{1,0:T(8,128)}, f32[1024,128]{1,0:T(8,128)}) async-done(((f32[128,1024]{1,0:T(8,128)}, f32[1024,1024]{1,0:T(8,128)}, f32[1024,128]{1,0:T(8,128)}), (f32[128,1024]{1,0:T(8,128)}, f32[1024,1024]{1,0:T(8,128)}, f32[1024,128]{1,0:T(8,128)})) %all-reduce.7.cloned.1.call-update) | async-done | bytes 5242896 | tf_op jit(solution)/shard_map/psum | solution.py:97
  244.2 0.0 all-reduce.5.cloned.1.call-update
  244.3 5.6 copy.33
  249.8 383.9 %all-reduce.5.cloned.1.call-done = (f32[128,1024]{1,0:T(8,128)}, f32[1024,1024]{1,0:T(8,128)}, f32[1024,128]{1,0:T(8,128)}) async-done(((f32[128,1024]{1,0:T(8,128)}, f32[1024,1024]{1,0:T(8,128)}, f32[1024,128]{1,0:T(8,128)}), (f32[128,1024]{1,0:T(8,128)}, f32[1024,1024]{1,0:T(8,128)}, f32[1024,128]{1,0:T(8,128)})) %all-reduce.5.cloned.1.call-update) | async-done | bytes 5242896 | tf_op jit(solution)/shard_map/psum | solution.py:96
  633.7 7.0 %multiply_subtract_fusion = f32[1024,1024]{1,0:T(8,128)} fusion(f32[1024,1024]{1,0:T(8,128)} %param.12, f32[1024,1024]{1,0:T(8,128)} %get-tuple-element.18), kind=kLoop, calls=%fused_computation.29 | loop fusion | flops 2097152 | bytes 12582912 | tf_op jit(solution)/shard_map/sub | solution.py:100
  640.7 0.8 multiply_subtract_fusion.1
  641.5 0.9 multiply_subtract_fusion.2
  (10 shorter events, 0.1 us)
Async XLA Ops:
  7.2 17.6 %copy-start.9 = (s32[384,1]{0,1:T(1,128)S(1)}, s32[384,1]{0,1:T(1,128)}, u32[]{:S(2)}) copy-start(s32[384,1]{0,1:T(1,128)} %param.14) | copy-start | bytes 4612
  7.2 17.8 %copy-start.7 = (s32[384]{0:T(512)S(1)}, s32[384]{0:T(512)}, u32[]{:S(2)}) copy-start(s32[384]{0:T(512)} %param.15) | copy-start | bytes 4612
  15.6 21.9 %collective-permute-start = (f32[128,2,512]{0,1,2:T(2,128)S(1)}, f32[128,2,512]{0,1,2:T(2,128)S(1)}, u32[]{:S(2)}, u32[]{:S(2)}) collective-permute-start(f32[128,2,512]{0,1,2:T(2,128)S(1)} %get-tuple-element.31), channel_id=1, source_target_pairs={{0,4},{4,8},{8,12},{12,16},{16,20},{20,24},{24,28},{28,32},{32,36}... | collective-permute-start | bytes 1572872 | tf_op jit(solution)/shard_map/ppermute | solution.py:18
  18.8 24.4 %collective-permute-start.1 = (f32[128,2,512]{0,1,2:T(2,128)S(1)}, f32[128,2,512]{0,1,2:T(2,128)S(1)}, u32[]{:S(2)}, u32[]{:S(2)}) collective-permute-start(f32[128,2,512]{0,1,2:T(2,128)S(1)} %get-tuple-element.32), channel_id=1, source_target_pairs={{4,0},{8,4},{12,8},{16,12},{20,16},{24,20},{28,24},{32,28},{36,32}... | collective-permute-start | bytes 1572872 | tf_op jit(solution)/shard_map/ppermute | solution.py:19
  43.9 14.3 %collective-permute-start.2 = (f32[128,20,2]{0,1,2:T(8,128)S(1)}, f32[128,20,2]{0,1,2:T(8,128)S(1)}, u32[]{:S(2)}, u32[]{:S(2)}) collective-permute-start(f32[128,20,2]{0,1,2:T(8,128)S(1)} %get-tuple-element.29), channel_id=1, source_target_pairs={{0,1},{1,2},{2,3},{3,0},{4,5},{5,6},{6,7},{7,4},{8,9},{9,10},{10,1... | collective-permute-start | bytes 61448 | tf_op jit(solution)/shard_map/ppermute | solution.py:18
  44.0 14.2 %collective-permute-start.3 = (f32[128,20,2]{0,1,2:T(8,128)S(1)}, f32[128,20,2]{0,1,2:T(8,128)S(1)}, u32[]{:S(2)}, u32[]{:S(2)}) collective-permute-start(f32[128,20,2]{0,1,2:T(8,128)S(1)} %get-tuple-element.30), channel_id=1, source_target_pairs={{1,0},{2,1},{3,2},{0,3},{5,4},{6,5},{7,6},{4,7},{9,8},{10,9},{11,1... | collective-permute-start | bytes 61448 | tf_op jit(solution)/shard_map/ppermute | solution.py:19
  47.4 35.1 %all-to-all-start = ((bf16[32,128,128]{2,1,0:T(8,128)(2,1)}), bf16[32,128,128]{2,1,0:T(8,128)(2,1)}, u32[]{:S(2)}, u32[]{:S(2)}) async-start(bf16[32,128,128]{2,1,0:T(8,128)(2,1)} %copy.30), calls=%async_computation | async-start | bytes 2097152 | tf_op jit(solution)/shard_map/all_to_all | solution.py:86
  58.2 4.3 copy-start
  58.2 4.3 copy-start.8
  80.7 30.5 %copy-start.4 = (f32[128,1024]{1,0:T(8,128)S(1)}, f32[128,1024]{1,0:T(8,128)}, u32[]{:S(2)}) copy-start(f32[128,1024]{1,0:T(8,128)} %param.11) | copy-start | bytes 1572868
  82.5 27.9 %all-to-all-start.1 = ((bf16[32,128,128]{2,1,0:T(8,128)(2,1)}), bf16[32,128,128]{2,1,0:T(8,128)(2,1)S(1)}, u32[]{:S(2)}, u32[]{:S(2)}) async-start(bf16[32,128,128]{2,1,0:T(8,128)(2,1)} %copy.32), calls=%async_computation.1 | async-start | bytes 2097152 | tf_op jit(solution)/shard_map/all_to_all | solution.py:87
  92.3 151.9 %all-reduce.7.cloned.1.call-start = ((), (), s32[]{:S(2)}) async-start(), calls=%async_computation.3 | async-start | bytes 10485760 | tf_op jit(solution)/shard_map/psum | solution.py:97
  111.0 2.2 copy-start.2
  113.2 10.1 %copy-start.1 = (f32[1536,1024]{1,0:T(8,128)}, f32[1536,1024]{1,0:T(8,128)S(1)}, u32[]{:S(2)}) copy-start(f32[1536,1024]{1,0:T(8,128)S(1)} %fusion.18) | copy-start | bytes 18874372
  113.2 4.5 copy-start.3
  123.3 1.7 copy-start.10
  140.7 493.0 %all-reduce.5.cloned.1.call-start = ((), (), s32[]{:S(2)}) async-start(), calls=%async_computation.2 | async-start | bytes 10485760 | tf_op jit(solution)/shard_map/psum | solution.py:96
  633.7 7.0 %copy-start.6 = (f32[1024,128]{1,0:T(8,128)S(1)}, f32[1024,128]{1,0:T(8,128)}, u32[]{:S(2)}) copy-start(f32[1024,128]{1,0:T(8,128)} %get-tuple-element.19) | copy-start | bytes 1572868
  633.7 7.8 %copy-start.5 = (f32[128,1024]{1,0:T(8,128)S(1)}, f32[128,1024]{1,0:T(8,128)}, u32[]{:S(2)}) copy-start(f32[128,1024]{1,0:T(8,128)} %get-tuple-element.17) | copy-start | bytes 1572868
Sparse Core Ops, SparseCore 0:
  140.8 103.3 all-reduce.6
  247.0 386.6 all-reduce.4
